TPU v7x, 128 devices: a whole 4x4x4 slice. The times are simulated.
128 devices in a mesh: frames: 32 (over x, z, core), heads: 4 (over y).
Axes of the slice: x: 4, y: 4, z: 4, core: 2. Of those that a mesh axis runs over, the one named last changes fastest.
Arguments:
- queries: bfloat16 [32768, 2560], P('frames', 'heads'), may hold values from -6 to 6, as said below
- keys: bfloat16 [32768, 2560], P('frames', 'heads'), may hold values from -6 to 6, as said below
- values: bfloat16 [32768, 2560], P('frames', 'heads'), may hold values from -6 to 6
- block_ids: int32 [256, 4], replicated, may hold values from 0 to 255, as said below
- counts: int32 [256], P('frames'), may hold values from 1 to 4
- w_out: bfloat16 [2560, 5120], P('heads'), may hold values from -0.125 to 0.125
Outputs:
- projected: bfloat16 [32768, 5120], P('frames', 'heads')
Inputs may be any that keep to these rules, and one draw needn't show every extreme that they name: `block_ids`: block j is held by index j // 8 of frames. Counted with repeats, the entries of the 8 query blocks of one index of frames name at most 2 blocks held by any one index, and exactly 2 held by some index. Entries of a row may repeat. `queries`: drawn in float32 and rounded once. `keys`: drawn in float32 and rounded once.
All inputs are finite; a program needn't handle non-finite values.
Results may differ from a plain program's by a relative error of at most 0.0052.
Values may be sent and summed in bfloat16 or wider, within the bound.
A program may use at most 192 MiB of HBM per device.

v0:
```python
import jax
import jax.numpy as jnp
from jax import lax
from jax.sharding import PartitionSpec as P

DH = 128
TILE = 128


def in_order(tiles, dim):
    tiles = jnp.moveaxis(tiles, 0, dim)
    dims = tiles.shape
    return tiles.reshape(*dims[:dim], dims[dim] * dims[dim + 1], *dims[dim + 2 :])


def sent_to_all(array, axis):
    devices = lax.axis_size(axis)
    return lax.all_to_all(
        jnp.broadcast_to(array[None], (devices, *array.shape)), axis, 0, 0, tiled=True
    )


def collect(array, axis, dim):
    return in_order(sent_to_all(array, axis), dim)


def shards(queries, keys, values, block_ids, counts, w_out):
    frame_count = lax.axis_size("frames")
    here_index = lax.axis_index("frames")
    tokens_here, width = queries.shape
    blocks = tokens_here // TILE
    select = block_ids.shape[1]
    heads_here = width // DH
    requests = blocks * select
    capacity = max(2, (requests + frame_count - 1) // frame_count)
    inv_root = 1.0 / DH**0.5
    owner_all = (block_ids // blocks).reshape(frame_count, requests)
    local_all = (block_ids % blocks).reshape(frame_count, requests)
    is_mine = owner_all == here_index
    mine_count = is_mine.astype(jnp.int32)
    slot_rank = jnp.cumsum(mine_count, axis=1) - mine_count
    slot_hit = is_mine[:, :, None] & (
        slot_rank[:, :, None] == jnp.arange(capacity, dtype=jnp.int32)[None, None, :]
    )
    send_index = jnp.sum(jnp.where(slot_hit, local_all[:, :, None], 0), axis=1)
    key_tiles = keys.reshape(blocks, TILE, width)
    value_tiles = values.reshape(blocks, TILE, width)
    send_keys = jnp.take(key_tiles, send_index.reshape(-1), axis=0).reshape(
        frame_count, capacity, TILE, width
    )
    send_values = jnp.take(value_tiles, send_index.reshape(-1), axis=0).reshape(
        frame_count, capacity, TILE, width
    )
    got_keys, got_values = (
        lax.all_to_all(send_keys, "frames", split_axis=0, concat_axis=0, tiled=True),
        lax.all_to_all(send_values, "frames", split_axis=0, concat_axis=0, tiled=True),
    )
    my_blocks = lax.dynamic_slice_in_dim(block_ids, here_index * blocks, blocks, 0).reshape(
        requests
    )
    my_owner = my_blocks // blocks
    positions = jnp.arange(requests, dtype=jnp.int32)
    earlier = (my_owner[None, :] == my_owner[:, None]) & (positions[None, :] < positions[:, None])
    my_rank = jnp.sum(earlier.astype(jnp.int32), axis=1)
    flat_slot = my_owner * capacity + my_rank
    chosen_keys = jnp.take(got_keys.reshape(frame_count * capacity, TILE, width), flat_slot, axis=0)
    chosen_values = jnp.take(
        got_values.reshape(frame_count * capacity, TILE, width), flat_slot, axis=0
    )
    chosen_keys = chosen_keys.reshape(blocks, select, TILE, width)
    chosen_values = chosen_values.reshape(blocks, select, TILE, width)
    keyset_k = jnp.concatenate([key_tiles[:, None], chosen_keys], 1).reshape(
        blocks, (select + 1) * TILE, heads_here, DH
    )
    keyset_v = jnp.concatenate([value_tiles[:, None], chosen_values], 1).reshape(
        blocks, (select + 1) * TILE, heads_here, DH
    )
    query_tiles = queries.reshape(blocks, TILE, heads_here, DH)
    scores = (
        jnp.einsum("bqhd,bkhd->bhqk", query_tiles, keyset_k, preferred_element_type=jnp.float32)
        * inv_root
    )
    allowed = jnp.concatenate(
        [jnp.ones((blocks, 1), bool), jnp.arange(select)[None, :] < counts[:, None]], axis=1
    )
    key_allowed = jnp.repeat(allowed, TILE, axis=1)
    scores = jnp.where(key_allowed[:, None, None, :], scores, -jnp.inf)
    row_max = jnp.max(scores, axis=-1, keepdims=True)
    probs = jnp.exp(scores - row_max)
    denom_sum = jnp.sum(probs, axis=-1)
    weights = probs.astype(jnp.bfloat16)
    mixed = jnp.einsum("bhqk,bkhd->bqhd", weights, keyset_v, preferred_element_type=jnp.float32)
    mixed = mixed / jnp.transpose(denom_sum, (0, 2, 1))[:, :, :, None]
    attn = mixed.astype(jnp.bfloat16).reshape(tokens_here, width)
    all_rows = lax.all_to_all(w_out, "heads", split_axis=1, concat_axis=0, tiled=True)
    return jnp.dot(collect(attn, "heads", 1), all_rows, preferred_element_type=jnp.float32).astype(
        jnp.bfloat16
    )


def solution(mesh):
    placed = (
        P("frames", "heads"),
        P("frames", "heads"),
        P("frames", "heads"),
        P(),
        P("frames"),
        P("heads", None),
    )
    return jax.shard_map(
        shards, mesh=mesh, in_specs=placed, out_specs=P("frames", "heads"), check_vma=False
    )
```

profile of v0, /device:TPU:36, one launch (start us, length us, event | category | flops | bytes accessed | tf_op | source)
XLA Modules:
  0.0 483.7 jit_solution(2589300470262201778)
XLA Ops:
  0.7 0.7 fusion.27
  2.5 7.8 %gather_fusion = bf16[64,128,640]{2,1,0:T(8,128)(2,1)} fusion(bf16[8,128,640]{2,1,0:T(8,128)(2,1)} %bitcast.55, s32[1024]{0:T(1024)S(1)} %pad_clamp_fusion.1), kind=kCustom, calls=%fused_computation.clone | custom fusion | bytes 20971776 | tf_op jit(solution)/shard_map/jit(_take)/gather | solution.py:51
  10.3 6.5 %gather_fusion.2 = bf16[64,128,640]{2,1,0:T(8,128)(2,1)} fusion(bf16[8,128,640]{2,1,0:T(8,128)(2,1)S(1)} %bitcast.53, s32[1024]{0:T(1024)S(1)} %pad_clamp_fusion.1), kind=kCustom, calls=%fused_computation.2.clone | custom fusion | bytes 20971776 | tf_op jit(solution)/shard_map/jit(_take)/gather | solution.py:48
  16.7 13.2 %broadcast_select_fusion.1 = (bf16[64,128,640]{2,1,0:T(8,128)(2,1)S(1)}, bf16[64,128,640]{2,1,0:T(8,128)(2,1)}) fusion(bf16[64,128,640]{2,1,0:T(8,128)(2,1)} %gather_fusion, pred[64]{0:T(512)(128)(4,1)S(1)} %compare_and_fusion.1, bf16[64,128,640]{2,1,0:T(8,128)(2,1)} %gather_fusion.2), kind=kLoop, calls=%fused_computation.9 | loop fusion | flops 10485760 | bytes 41943104 | tf_op jit(solution)/shard_map/jit(_take)/select_n | solution.py:51
  29.9 123.0 %all_to_all.31 = bf16[32,2,128,640]{3,2,1,0:T(8,128)(2,1)} all-to-all(bf16[32,2,128,640]{3,2,1,0:T(8,128)(2,1)S(1)} %bitcast.58), channel_id=1, replica_groups=mesh['frames'=32,'heads'=4] {'frames'}, dimensions={0} | all-to-all | bytes 20971520 | tf_op jit(solution)/shard_map/all_to_all | solution.py:56
  152.9 8.1 %all-to-all-start.1 = ((bf16[32,2,128,640]{3,2,1,0:T(8,128)(2,1)}), bf16[32,2,128,640]{3,2,1,0:T(8,128)(2,1)}, u32[]{:S(2)}, u32[]{:S(2)}) async-start(bf16[32,2,128,640]{3,2,1,0:T(8,128)(2,1)} %bitcast.57), calls=%async_computation.1 | async-start | bytes 20971520 | tf_op jit(solution)/shard_map/all_to_all | solution.py:55
  161.2 3.1 reshape.198
  164.3 9.5 %copy.38 = bf16[640,5120]{0,1:T(8,128)(2,1)} copy(bf16[640,5120]{1,0:T(8,128)(2,1)} %param.15) | data formatting | bytes 13107200 | tf_op args[5]
  173.8 9.5 %copy.39 = bf16[640,4,1280]{2,0,1:T(8,128)(2,1)} copy(bf16[640,4,1280]{0,2,1:T(8,128)(2,1)} %bitcast.59) | data formatting | bytes 13107200 | tf_op jit(solution)/shard_map/all_to_all | solution.py:95
  183.7 7.5 %gather_fusion.1 = bf16[32,128,640]{2,1,0:T(8,128)(2,1)} fusion(bf16[64,128,640]{2,1,0:T(8,128)(2,1)} %bitcast.60, s32[1024]{0:T(1024)S(1)} %pad_clamp_fusion), kind=kCustom, calls=%fused_computation.1.clone | custom fusion | bytes 10485888 | tf_op jit(solution)/shard_map/jit(_take)/gather | solution.py:67
  191.2 132.2 %all-to-all-done.1 = bf16[32,2,128,640]{3,2,1,0:T(8,128)(2,1)} async-done(((bf16[32,2,128,640]{3,2,1,0:T(8,128)(2,1)}), bf16[32,2,128,640]{3,2,1,0:T(8,128)(2,1)}, u32[]{:S(2)}, u32[]{:S(2)}) %all-to-all-start.1) | async-done | bytes 10485792 | tf_op jit(solution)/shard_map/all_to_all | solution.py:55
  323.3 5.5 %all-to-all-start.3 = ((bf16[640,4,1280]{2,0,1:T(8,128)(2,1)}), bf16[640,4,1280]{2,0,1:T(8,128)(2,1)}, u32[]{:S(2)}, u32[]{:S(2)}) async-start(bf16[640,4,1280]{2,0,1:T(8,128)(2,1)} %copy.39), calls=%async_computation.3 | async-start | bytes 13107200 | tf_op jit(solution)/shard_map/all_to_all | solution.py:95
  328.8 7.5 %gather_fusion.3 = bf16[32,128,640]{2,1,0:T(8,128)(2,1)} fusion(bf16[64,128,640]{2,1,0:T(8,128)(2,1)} %bitcast.10, s32[1024]{0:T(1024)S(1)} %pad_clamp_fusion), kind=kCustom, calls=%fused_computation.3.clone | custom fusion | bytes 10485888 | tf_op jit(solution)/shard_map/jit(_take)/gather | solution.py:66
  336.3 9.2 %broadcast_select_fusion.3 = (bf16[32,128,640]{2,1,0:T(8,128)(2,1)}, bf16[32,128,640]{2,1,0:T(8,128)(2,1)}) fusion(bf16[32,128,640]{2,1,0:T(8,128)(2,1)} %gather_fusion.1, pred[32]{0:T(512)(128)(4,1)S(1)} %get-tuple-element.6, bf16[32,128,640]{2,1,0:T(8,128)(2,1)} %gather_fusion.3), kind=kLoop, calls=%fused_computation.27 | loop fusion | flops 5242880 | bytes 20971552 | tf_op jit(solution)/shard_map/jit(_take)/select_n | solution.py:67
  345.5 5.9 %pad_maximum_fusion.1 = bf16[8,5,128,640]{3,2,1,0:T(8,128)(2,1)} fusion(bf16[8,4,128,640]{3,2,1,0:T(8,128)(2,1)} %bitcast.62, bf16[8,1,128,640]{3,2,1,0:T(8,128)(2,1)S(1)} %bitcast.54), kind=kLoop, calls=%fused_computation.14 | loop fusion | flops 3276800 | bytes 13107200 | tf_op jit(solution)/shard_map/concatenate | solution.py:72
  351.3 15.1 %reshape.151 = bf16[8,640,5,128]{3,2,1,0:T(8,128)(2,1)} reshape(bf16[8,5,128,640]{3,2,1,0:T(8,128)(2,1)} %pad_maximum_fusion.1) | data formatting | bytes 13107200 | tf_op jit(solution)/shard_map/reshape | solution.py:72
  366.5 5.9 %pad_maximum_fusion = bf16[8,5,128,640]{3,2,1,0:T(8,128)(2,1)} fusion(bf16[8,4,128,640]{3,2,1,0:T(8,128)(2,1)} %bitcast.61, bf16[8,1,128,640]{3,2,1,0:T(8,128)(2,1)S(1)} %bitcast.56), kind=kLoop, calls=%fused_computation.13 | loop fusion | flops 3276800 | bytes 13107200 | tf_op jit(solution)/shard_map/concatenate | solution.py:75
  372.3 15.1 %reshape.146 = bf16[8,640,5,128]{3,2,1,0:T(8,128)(2,1)} reshape(bf16[8,5,128,640]{3,2,1,0:T(8,128)(2,1)} %pad_maximum_fusion) | data formatting | bytes 13107200 | tf_op jit(solution)/shard_map/reshape | solution.py:75
  387.5 6.4 %bitcast_reduce_fusion = (f32[8,5,128]{2,1,0:T(8,128)S(1)}, f32[8,5,640,128]{3,2,1,0:T(8,128)S(1)}) fusion(pred[8,640]{1,0:T(8,128)(4,1)S(1)} %broadcast_bitcast_fusion, bf16[8,128,5,128]{3,2,1,0:T(8,128)(2,1)S(1)} %reshape.198, bf16[8,640,5,128]{3,2,1,0:T(8,128)(2,1)} %reshape.151), kind=kOutput, calls=%fused_computation.5 | convolution fusion | flops 848686080 | bytes 20997120 | tf_op jit(solution)/shard_map/bqhd,bkhd->bhqk/dot_general | solution.py:80
  393.8 3.0 fusion.1
  396.8 8.2 %fusion.19 = bf16[8,128,5,128]{1,3,2,0:T(8,128)(2,1)S(1)} fusion(f32[8,5,640,128]{3,2,1,0:T(8,128)S(1)} %get-tuple-element.14, f32[8,5,128]{2,1,0:T(8,128)S(1)} %get-tuple-element.13, pred[8,640]{1,0:T(8,128)(4,1)S(1)} %broadcast_bitcast_fusion, bf16[8,640,5,128]{3,2,1,0:T(8,128)(2,1)} %reshape.146, f32[8,128,5]{1,2,0:T(8,128)S(1)} %bitcast.65), kind=kOutput, calls=%fused_computation.29 | convolution fusion | flops 853278720 | bytes 21017600 | tf_op jit(solution)/shard_map/bhqk,bkhd->bqhd/dot_general | solution.py:92
  405.0 2.5 copy.43
  408.2 64.0 %all_to_all.32 = bf16[4,1024,640]{2,1,0:T(8,128)(2,1)S(1)} all-to-all(bf16[4,1024,640]{2,1,0:T(8,128)(2,1)S(1)} %broadcast_in_dim.75), channel_id=1, replica_groups=mesh['frames'=32,'heads'=4] {'heads'}, dimensions={0} | all-to-all | bytes 10485760 | tf_op jit(solution)/shard_map/all_to_all | solution.py:18
  472.2 11.5 %bitcast_convert_fusion = bf16[1024,1280]{1,0:T(8,128)(2,1)} fusion(bf16[640,4,1280]{2,0,1:T(8,128)(2,1)} %all-to-all-done.3, bf16[4,1024,640]{2,1,0:T(8,128)(2,1)S(1)} %all_to_all.32), kind=kOutput, calls=%fused_computation.24 | convolution fusion | flops 6712197120 | bytes 14417920 | tf_op jit(solution)/shard_map/dot_general | solution.py:96
  (35 shorter events, 3.0 us)
Async XLA Ops:
  2.5 7.8 %copy-start = (bf16[1024,640]{1,0:T(8,128)(2,1)S(1)}, bf16[1024,640]{1,0:T(8,128)(2,1)}, u32[]{:S(2)}) copy-start(bf16[1024,640]{1,0:T(8,128)(2,1)} %param.11) | copy-start | bytes 3932164
  152.9 8.1 %copy-start.2 = (s32[256,4]{0,1:T(4,128)S(1)}, s32[256,4]{0,1:T(4,128)}, u32[]{:S(2)}) copy-start(s32[256,4]{0,1:T(4,128)} %param.13) | copy-start | bytes 12292
  152.9 170.5 %all-to-all-start.1 = ((bf16[32,2,128,640]{3,2,1,0:T(8,128)(2,1)}), bf16[32,2,128,640]{3,2,1,0:T(8,128)(2,1)}, u32[]{:S(2)}, u32[]{:S(2)}) async-start(bf16[32,2,128,640]{3,2,1,0:T(8,128)(2,1)} %bitcast.57), calls=%async_computation.1 | async-start | bytes 20971520 | tf_op jit(solution)/shard_map/all_to_all | solution.py:55
  173.8 9.5 %copy-start.3 = (s32[8]{0:T(128)S(1)}, s32[8]{0:T(128)}, u32[]{:S(2)}) copy-start(s32[8]{0:T(128)} %param.14) | copy-start | bytes 100
  323.3 84.5 %all-to-all-start.3 = ((bf16[640,4,1280]{2,0,1:T(8,128)(2,1)}), bf16[640,4,1280]{2,0,1:T(8,128)(2,1)}, u32[]{:S(2)}, u32[]{:S(2)}) async-start(bf16[640,4,1280]{2,0,1:T(8,128)(2,1)} %copy.39), calls=%async_computation.3 | async-start | bytes 13107200 | tf_op jit(solution)/shard_map/all_to_all | solution.py:95
  351.3 15.1 %copy-start.1 = (bf16[1024,640]{1,0:T(8,128)(2,1)S(1)}, bf16[1024,640]{1,0:T(8,128)(2,1)}, u32[]{:S(2)}) copy-start(bf16[1024,640]{1,0:T(8,128)(2,1)} %param.12) | copy-start | bytes 3932164
where the time goes:
time: 485 us; the launch traced here: 484 us
  blocking collectives  187 us (39%)
  waiting for transfers between devices  132 us (27%)
  local copies, waits for them, and re-layouts  85.8 us (18%)
  other arithmetic  39 us (8%)
  matrix products  26 us (5%)
  starting transfers between devices  13.5 us (3%)
    all_to_all x1, waiting for transfers between devices, shards(): lax.all_to_all(send_keys, 'frames', split_axis=0, concat_axis=0, tiled=True)  132 us
    all_to_all x1, blocking collectives, shards(): lax.all_to_all(send_values, 'frames', split_axis=0, concat_axis=0, tiled=...  123 us
    all_to_all x1, blocking collectives, sent_to_all(): lax.all_to_all(jnp.broadcast_to(array[None], (devices, *array.shape)), ax...  64 us
    reshape x1, local copies, waits for them, and re-layouts, shards(): jnp.concatenate([key_tiles[:, None], chosen_keys], 1)  15.1 us
    reshape x1, local copies, waits for them, and re-layouts, shards(): jnp.concatenate([value_tiles[:, None], chosen_values], 1)  15.1 us
    select_n x2, other arithmetic, shards(): jnp.take(value_tiles, send_index.reshape(-1), axis=0)  13.2 us
    dot_general x1, matrix products, shards(): jnp.dot(collect(attn, 'heads', 1), all_rows, preferred_element_type=jnp.f...  11.5 us
    unnamed x10, local copies, waits for them, and re-layouts  9.76 us
  transfers between devices with their start and end apart: 2, of which 1 were waited for; matrix products, arithmetic and copies ran while one was open for 23% of the time, Pallas kernels for 0%

commit v1 on v0

v1 whole, which is shorter than its diff:
```python
import math

import jax
import jax.numpy as jnp
from jax import lax
from jax.experimental import pallas as pl
from jax.experimental.pallas import tpu as pltpu
from jax.sharding import PartitionSpec as P

DH = 128
TILE = 128
SEL = 4
RING = 4
HEADS_HERE = 5
BLOCKS = 8
TOK = BLOCKS * TILE
HALF = TOK // 2
WIDTH = HEADS_HERE * DH
FEAT = 1280
NEG = -1e30
TO_LOG2 = math.log2(math.e) / math.sqrt(DH)


def all_waited(copies):
    for copy in copies:
        copy.wait_send()


def kernel(
    ids, cnt, q_in, k_in, v_in, w_in, out,
    QB, CB, OB, OWN, RLY, OIN, LB, LRLY, LIN, AT, W, ACC,
    send_sem, recv_sem, local_sem, *kv_bufs,
):
    KB, VB = kv_bufs[:HEADS_HERE], kv_bufs[HEADS_HERE:]
    f = lax.axis_index("frames")
    py = lax.axis_index("heads")
    px = f // 8
    pz = (f // 2) % 4
    c = f % 2

    def frame(x, z, core):
        return (x * 4 + z) * 2 + core

    def up(p):
        return (p + 1) % 4

    def down(p):
        return (p + 3) % 4

    x_right, x_left = (frame(up(px), pz, c), py), (frame(down(px), pz, c), py)
    z_right, z_left = (frame(px, up(pz), c), py), (frame(px, down(pz), c), py)
    z_far = (frame(px, (pz + 2) % 4, c), py)
    y_right, y_left, y_far = (f, up(py)), (f, down(py)), (f, (py + 2) % 4)
    sibling = (frame(px, pz, 1 - c), py)
    partners = [x_right, x_left, z_right, z_left, z_far, y_right, y_left, y_far, sibling]

    barrier = pltpu.get_barrier_semaphore()
    for device in partners:
        pl.semaphore_signal(barrier, inc=1, device_id=device, device_id_type=MESH)
    pl.semaphore_wait(barrier, len(partners))

    used = [0]
    used_local = [0]
    sent = []

    def remote(src, dst, device):
        i = used[0]
        used[0] += 1
        return pltpu.make_async_remote_copy(
            src_ref=src, dst_ref=dst, send_sem=send_sem.at[i], recv_sem=recv_sem.at[i],
            device_id=device, device_id_type=MESH,
        )

    def local(src, dst):
        i = used_local[0]
        used_local[0] += 1
        return pltpu.make_async_copy(src, dst, local_sem.at[i])

    def go(copies):
        for copy in copies:
            copy.start()
            sent.append(copy)

    def cols(h):
        return pl.ds(h * DH, DH)

    heads = range(HEADS_HERE)
    lo, hi = pl.ds(0, HALF), pl.ds(HALF, HALF)

    def slot(s, part=None):
        if part is None:
            return pl.ds(s * BLOCKS, BLOCKS)
        return pl.ds(s * BLOCKS + part * (BLOCKS // 2), BLOCKS // 2)

    kv = []
    for h in heads:
        hc = cols(h)
        first, fwd, sib_own, sib_near, sib_far, own = [], [], [], [], [], []
        for src, buf in ((k_in, KB[h]), (v_in, VB[h])):
            mine = src.at[:, :, hc]
            first.append((remote(mine, buf.at[slot(2)], x_right),
                          remote(mine, buf.at[slot(6)], x_left)))
            fwd.append((remote(buf.at[slot(2, 0)], buf.at[slot(4, 0)], x_right),
                        remote(buf.at[slot(6, 1)], buf.at[slot(4, 1)], x_left)))
            sib_own.append(remote(mine, buf.at[slot(1)], sibling))
            sib_near.append((remote(buf.at[slot(2)], buf.at[slot(3)], sibling),
                             remote(buf.at[slot(6)], buf.at[slot(7)], sibling)))
            sib_far.append((remote(buf.at[slot(4, 0)], buf.at[slot(5, 0)], sibling),
                            remote(buf.at[slot(4, 1)], buf.at[slot(5, 1)], sibling)))
            own.append(local(mine, buf.at[slot(0)]))
        kv.append((first, fwd, sib_own, sib_near, sib_far, own))

    def ring(src, dst_near, dst_far, device_right, device_left, hc):
        first = (remote(src, dst_near[0].at[:, hc], device_right),
                 remote(src, dst_near[1].at[:, hc], device_left))
        fwd = (remote(dst_near[0].at[lo, hc], dst_far.at[lo, hc], device_right),
               remote(dst_near[1].at[hi, hc], dst_far.at[hi, hc], device_left))
        return first, fwd

    qs = []
    for h in heads:
        mine = q_in.at[:, cols(h)]
        first, fwd = ring(mine, (QB.at[1], QB.at[3]), QB.at[2], z_right, z_left, cols(h))
        qs.append((first, fwd, local(mine, QB.at[0, :, cols(h)])))
    ys = [ring(AT.at[0, :, cols(h)], (AT.at[1], AT.at[3]), AT.at[2], y_right, y_left, cols(h))
          for h in heads]

    os = []
    for h in heads:
        hc = cols(h)
        relay = (remote(OB.at[2, lo, hc], RLY.at[0, :, hc], z_right),
                 remote(LB.at[2, h, pl.ds(0, 4)], LRLY.at[0, h], z_right),
                 remote(OB.at[2, hi, hc], RLY.at[1, :, hc], z_left),
                 remote(LB.at[2, h, pl.ds(4, 4)], LRLY.at[1, h], z_left))
        back = (remote(OB.at[3, :, hc], OIN.at[0, :, hc], z_right),
                remote(LB.at[3, h], LIN.at[0, h], z_right),
                remote(OB.at[1, :, hc], OIN.at[1, :, hc], z_left),
                remote(LB.at[1, h], LIN.at[1, h], z_left))
        os.append((relay, back))

    rows_w = pl.ds(pl.multiple_of(c * (WIDTH // 2), WIDTH // 2), WIDTH // 2)

    def w_cols(y):
        return pl.ds(pl.multiple_of(y * FEAT, FEAT), FEAT)

    w_first = [remote(w_in.at[rows_w, w_cols(dev[1])], W.at[s, rows_w, :], dev)
               for s, dev in ((1, y_right), (3, y_left), (2, y_far))]
    w_sib = [remote(W.at[s, rows_w, :], W.at[s, rows_w, :], sibling) for s in (1, 3, 2)]
    w_own = local(w_in.at[:, w_cols(py)], W.at[0])
    cnt_copies = [remote(cnt, CB.at[s], dev) for s, dev in ((1, z_right), (3, z_left), (2, z_far))]

    def issue(h):
        first, _, sib_own, _, _, own = kv[h]
        go(qs[h][0])
        for pair in first:
            go(pair)
        go(sib_own)
        for copy in own + [qs[h][2]]:
            copy.start()

    def forward(h):
        first, fwd, _, sib_near, _, _ = kv[h]
        for t in range(2):
            for side in range(2):
                first[t][side].wait_recv()
                go([fwd[t][side], sib_near[t][side]])
        for side in range(2):
            qs[h][0][side].wait_recv()
            go([qs[h][1][side]])

    def ready(h):
        _, fwd, sib_own, sib_near, sib_far, own = kv[h]
        for t in range(2):
            for side in range(2):
                fwd[t][side].wait_recv()
                go([sib_far[t][side]])
        for side in range(2):
            qs[h][1][side].wait_recv()
        for copy in own + [qs[h][2]]:
            copy.wait()
        for t in range(2):
            sib_own[t].wait_recv()
            for side in range(2):
                sib_near[t][side].wait_recv()
            for side in range(2):
                sib_far[t][side].wait_recv()

    eye = lax.broadcasted_iota(jnp.int32, (TILE, TILE), 0) == lax.broadcasted_iota(
        jnp.int32, (TILE, TILE), 1)

    def as_row(col):
        return jnp.sum(jnp.where(eye, col, 0.0), axis=0, keepdims=True)

    def as_col(row):
        return jnp.sum(jnp.where(eye, row, 0.0), axis=1, keepdims=True)

    def attend(r, h, j):
        hc = cols(h)
        q = QB[r, pl.ds(pl.multiple_of(j * TILE, TILE), TILE), hc]
        q_block = frame(px, (pz + 4 - r) % 4, c) * BLOCKS + j
        limit = CB[r, pl.ds(j, 1), :]
        scores, vals = [], []
        for s in range(SEL):
            block = ids[q_block * SEL + s]
            xs, zs, cs = block >> 6, (block >> 4) & 3, (block >> 3) & 1
            place = ((((px + 4 - xs) & 3) * 2 + ((cs + c) & 1)) * BLOCKS) + (block & 7)
            here = jnp.where(zs == pz, 0.0, NEG)
            bias = jnp.where(limit > s, here, NEG)
            k = KB[h][place]
            vals.append(VB[h][place])
            scores.append(lax.dot_general(q, k, (((1,), (1,)), ((), ())),
                                          preferred_element_type=jnp.float32) * TO_LOG2 + bias)
        if r == 0:
            vals.append(VB[h][j])
            scores.append(lax.dot_general(q, KB[h][j], (((1,), (1,)), ((), ())),
                                          preferred_element_type=jnp.float32) * TO_LOG2)
        top = scores[0]
        for t in scores[1:]:
            top = jnp.maximum(top, t)
        top = jnp.max(top, axis=1, keepdims=True)
        probs = [jnp.exp2(t - top) for t in scores]
        total = probs[0]
        for p in probs[1:]:
            total = total + p
        total = jnp.sum(total, axis=1, keepdims=True)
        o = jnp.dot(jnp.concatenate([p.astype(jnp.bfloat16) for p in probs], axis=1),
                    jnp.concatenate(vals, axis=0), preferred_element_type=jnp.float32)
        return o * (1.0 / total), top + jnp.log2(total)

    def merge(parts):
        top = parts[0][1]
        for _, l in parts[1:]:
            top = jnp.maximum(top, l)
        mass, o = 0.0, 0.0
        for po, l in parts:
            a = jnp.exp2(l - top)
            mass = mass + a
            o = o + po.astype(jnp.float32) * a
        return o * (1.0 / mass), top + jnp.log2(mass)

    def over(first_block, n, body):
        def pair(i, carry):
            for u in range(2):
                body(first_block + i * 2 + u)
            return carry
        lax.fori_loop(0, n // 2, pair, 0)

    def block_rows(j):
        return pl.ds(pl.multiple_of(j * TILE, TILE), TILE)

    def plain(r, h):
        def body(j):
            o, l = attend(r, h, j)
            OB[r, block_rows(j), cols(h)] = o.astype(jnp.bfloat16)
            LB[r, h, j] = as_row(l)
        return body

    def merged(r, h, side, first_block):
        def body(j):
            o, l = attend(r, h, j)
            o, l = merge([(o, l), (RLY[side, block_rows(j - first_block), cols(h)],
                                   as_col(LRLY[side, h, j - first_block]))])
            OB[r, block_rows(j), cols(h)] = o.astype(jnp.bfloat16)
            LB[r, h, j] = as_row(l)
        return body

    def own_part(h):
        def body(j):
            o, l = attend(0, h, j)
            OWN[block_rows(j), cols(h)] = o
            LB[0, h, j] = as_row(l)
        return body

    def final(h):
        def body(j):
            parts = [(OWN[block_rows(j), cols(h)], as_col(LB[0, h, j]))]
            for side in range(2):
                parts.append((OIN[side, block_rows(j), cols(h)], as_col(LIN[side, h, j])))
            o, _ = merge(parts)
            AT[0, block_rows(j), cols(h)] = o.astype(jnp.bfloat16)
        return body

    def y_forward(h):
        first, fwd = ys[h]
        for side in range(2):
            first[side].wait_recv()
            go([fwd[side]])

    def project(h):
        for side in range(2):
            ys[h][1][side].wait_recv()
        last = h == HEADS_HERE - 1
        tile_n, tile_m = 256, 256

        def one(i, carry):
            cs = pl.ds(pl.multiple_of(i * tile_n, tile_n), tile_n)
            rhs = jnp.concatenate([W[r, pl.ds(h * DH, DH), cs] for r in range(RING)], axis=0)
            for m in range(TOK // tile_m):
                rs = pl.ds(m * tile_m, tile_m)
                lhs = jnp.concatenate([AT[r, rs, cols(h)] for r in range(RING)], axis=1)
                term = jnp.dot(lhs, rhs, preferred_element_type=jnp.float32)
                if h > 0:
                    term = term + ACC[rs, cs]
                if last:
                    out[rs, cs] = term.astype(jnp.bfloat16)
                else:
                    ACC[rs, cs] = term
            return carry

        lax.fori_loop(0, FEAT // tile_n, one, 0)

    CB[0] = cnt[...]
    go(cnt_copies)
    issue(0)
    issue(1)
    go(w_first)
    w_own.start()
    for copy in cnt_copies:
        copy.wait_recv()
    forward(0)
    issue(2)
    for h in heads:
        ready(h)
        if h + 1 < HEADS_HERE:
            forward(h + 1)
        if h + 3 < HEADS_HERE:
            issue(h + 3)
        over(0, 8, plain(2, h))
        go(os[h][0])
        if h == 1:
            for a, b in zip(w_first, w_sib):
                a.wait_recv()
                go([b])
        if h > 0:
            y_forward(h - 1)
        over(0, 8, own_part(h))
        over(4, 4, plain(3, h))
        over(0, 4, plain(1, h))
        for copy in os[h][0]:
            copy.wait_recv()
        over(0, 4, merged(3, h, 0, 0))
        over(4, 4, merged(1, h, 1, 4))
        go(os[h][1])
        if h == 1:
            for copy in w_sib:
                copy.wait_recv()
            w_own.wait()
        if h > 0:
            project(h - 1)
        for copy in os[h][1]:
            copy.wait_recv()
        over(0, 8, final(h))
        go(ys[h][0])
    y_forward(HEADS_HERE - 1)
    project(HEADS_HERE - 1)
    all_waited(sent)


MESH = pl.DeviceIdType.MESH
N_REMOTE = 5 * (18 + 4 + 4 + 8) + 6 + 3
N_LOCAL = 5 * 3 + 1


def shards(queries, keys, values, block_ids, counts, w_out):
    ids = block_ids.reshape(-1)
    cnt = jnp.broadcast_to(counts[:, None], (BLOCKS, 128))
    vmem = pl.BlockSpec(memory_space=pltpu.VMEM)
    hbm = pl.BlockSpec(memory_space=pl.ANY)
    bf16, f32 = jnp.bfloat16, jnp.float32
    return pl.pallas_call(
        kernel,
        out_shape=jax.ShapeDtypeStruct((TOK, FEAT), bf16),
        in_specs=[pl.BlockSpec(memory_space=pltpu.SMEM), vmem, hbm, hbm, hbm, hbm],
        out_specs=vmem,
        scratch_shapes=[
            pltpu.VMEM((4, TOK, WIDTH), bf16),
            pltpu.VMEM((4, BLOCKS, 128), jnp.int32),
            pltpu.VMEM((4, TOK, WIDTH), bf16),
            pltpu.VMEM((TOK, WIDTH), f32),
            pltpu.VMEM((2, HALF, WIDTH), bf16),
            pltpu.VMEM((2, TOK, WIDTH), bf16),
            pltpu.VMEM((4, HEADS_HERE, BLOCKS, 1, 128), f32),
            pltpu.VMEM((2, HEADS_HERE, BLOCKS // 2, 1, 128), f32),
            pltpu.VMEM((2, HEADS_HERE, BLOCKS, 1, 128), f32),
            pltpu.VMEM((4, TOK, WIDTH), bf16),
            pltpu.VMEM((4, WIDTH, FEAT), bf16),
            pltpu.VMEM((TOK, FEAT), f32),
            pltpu.SemaphoreType.DMA((N_REMOTE,)),
            pltpu.SemaphoreType.DMA((N_REMOTE,)),
            pltpu.SemaphoreType.DMA((N_LOCAL,)),
        ] + [pltpu.VMEM((8 * BLOCKS, TILE, DH), bf16)] * (2 * HEADS_HERE),
        compiler_params=pltpu.CompilerParams(
            collective_id=0, has_side_effects=True, vmem_limit_bytes=67043328),
        name="sparse_attention",
    )(ids, cnt, queries, keys.reshape(BLOCKS, TILE, WIDTH), values.reshape(BLOCKS, TILE, WIDTH), w_out)


def solution(mesh):
    placed = (
        P("frames", "heads"),
        P("frames", "heads"),
        P("frames", "heads"),
        P(),
        P("frames"),
        P("heads", None),
    )
    return jax.shard_map(
        shards, mesh=mesh, in_specs=placed, out_specs=P("frames", "heads"), check_vma=False
    )
```

time: 485 us -> 191 us (0.39)
  the two profiles are of different devices: /device:TPU:36 before, /device:TPU:0 now
where the time goes in v1:
time: 191 us; the launch traced here: 188 us
  Pallas kernels  182 us (95%)
  local copies, waits for them, and re-layouts  6.23 us (3%)
    pallas_call x1, Pallas kernels, shards(): pl.pallas_call(kernel, out_shape=jax.ShapeDtypeStruct((TOK, FEAT), bf16),...  182 us
    unnamed x2, local copies, waits for them, and re-layouts  4.21 us

profile of v1, /device:TPU:0, one launch (start us, length us, event | category | flops | bytes accessed | tf_op | source)
XLA Modules:
  0.0 188.3 jit_solution(11210425181848330000)
XLA Ops:
  0.0 1.3 broadcast_in_dim.2.cnt
  1.3 0.8 copy.7
  2.1 0.7 reshape.10.ids
  2.8 182.1 %sparse_attention.1 = bf16[1024,1280]{1,0:T(8,128)(2,1)} custom-call(s32[1024]{0:T(1024)} %reshape.10.ids, s32[8,128]{1,0:T(8,128)} %broadcast_in_dim.2.cnt, bf16[1024,640]{1,0:T(8,128)(2,1)} %q_in.1, bf16[8,128,640]{2,1,0:T(8,128)(2,1)} %bitcast.2, bf16[8,128,640]{2,1,0:T(8,128)(2,1)} %bitcast.3, bf16[640,5120]{1,0:T(8,128)(2,1)} %w_in.1), custom_call_target="tpu_custom_call" | custom-call | tf_op jit(solution)/shard_map/sparse_attention/pallas_call | solution.py:370
  184.9 3.4 %copy.9 = bf16[1024,1280]{1,0:T(8,128)(2,1)} copy(bf16[1024,1280]{1,0:T(8,128)(2,1)} %sparse_attention.1) | data formatting | bytes 5242880

commit v2 on v1

v2 whole, which is shorter than its diff:
```python
import math

import jax
import jax.numpy as jnp
from jax import lax
from jax.experimental import pallas as pl
from jax.experimental.pallas import tpu as pltpu
from jax.sharding import PartitionSpec as P

DH = 128
TILE = 128
SEL = 4
RING = 4
HEADS_HERE = 5
BLOCKS = 8
TOK = BLOCKS * TILE
HALF = TOK // 2
WIDTH = HEADS_HERE * DH
FEAT = 1280
NEG = -1e30
TO_LOG2 = math.log2(math.e) / math.sqrt(DH)


def all_waited(copies):
    for copy in copies:
        copy.wait_send()


def kernel(
    ids, cnt, q_in, k_in, v_in, w_in, out,
    QB, CB, VIN, OB, OWN, RLY, OIN, LB, LRLY, LIN, AT, W, ACC,
    send_sem, recv_sem, local_sem, *kv_bufs,
):
    KB, VB = kv_bufs[:HEADS_HERE], kv_bufs[HEADS_HERE:]
    f = lax.axis_index("frames")
    py = lax.axis_index("heads")
    px = f // 8
    pz = (f // 2) % 4
    c = f % 2

    def frame(x, z, core):
        return (x * 4 + z) * 2 + core

    def up(p):
        return (p + 1) % 4

    def down(p):
        return (p + 3) % 4

    x_right, x_left = (frame(up(px), pz, c), py), (frame(down(px), pz, c), py)
    z_right, z_left = (frame(px, up(pz), c), py), (frame(px, down(pz), c), py)
    z_far = (frame(px, (pz + 2) % 4, c), py)
    y_right, y_left, y_far = (f, up(py)), (f, down(py)), (f, (py + 2) % 4)
    sibling = (frame(px, pz, 1 - c), py)
    partners = [x_right, x_left, z_right, z_left, z_far, y_right, y_left, y_far, sibling]

    barrier = pltpu.get_barrier_semaphore()
    for device in partners:
        pl.semaphore_signal(barrier, inc=1, device_id=device, device_id_type=MESH)
    pl.semaphore_wait(barrier, len(partners))

    used = [0]
    used_local = [0]
    sent = []

    def remote(src, dst, device):
        i = used[0]
        used[0] += 1
        return pltpu.make_async_remote_copy(
            src_ref=src, dst_ref=dst, send_sem=send_sem.at[i], recv_sem=recv_sem.at[i],
            device_id=device, device_id_type=MESH,
        )

    def local(src, dst):
        i = used_local[0]
        used_local[0] += 1
        return pltpu.make_async_copy(src, dst, local_sem.at[i])

    def go(copies):
        for copy in copies:
            copy.start()
            sent.append(copy)

    def cols(h):
        return pl.ds(h * DH, DH)

    heads = range(HEADS_HERE)
    lo, hi = pl.ds(0, HALF), pl.ds(HALF, HALF)

    def slot(s, part=None):
        if part is None:
            return pl.ds(s * BLOCKS, BLOCKS)
        return pl.ds(s * BLOCKS + part * (BLOCKS // 2), BLOCKS // 2)

    kv = []
    for h in heads:
        hc = cols(h)
        first, fwd, sib_own, sib_near, sib_far, own = [], [], [], [], [], []
        for mine, buf in ((k_in.at[:, :, hc], KB[h]), (VB[h].at[slot(0)], VB[h])):
            first.append((remote(mine, buf.at[slot(2)], x_right),
                          remote(mine, buf.at[slot(6)], x_left)))
            fwd.append((remote(buf.at[slot(2, 0)], buf.at[slot(4, 0)], x_right),
                        remote(buf.at[slot(6, 1)], buf.at[slot(4, 1)], x_left)))
            sib_own.append(remote(mine, buf.at[slot(1)], sibling))
            sib_near.append((remote(buf.at[slot(2)], buf.at[slot(3)], sibling),
                             remote(buf.at[slot(6)], buf.at[slot(7)], sibling)))
            sib_far.append((remote(buf.at[slot(4, 0)], buf.at[slot(5, 0)], sibling),
                            remote(buf.at[slot(4, 1)], buf.at[slot(5, 1)], sibling)))
        own.append(local(k_in.at[:, :, hc], KB[h].at[slot(0)]))
        kv.append((first, fwd, sib_own, sib_near, sib_far, own))

    def ring(src, buf, h, device_right, device_left):
        first = (remote(src, buf.at[1, h], device_right), remote(src, buf.at[3, h], device_left))
        fwd = (remote(buf.at[1, h, lo], buf.at[2, h, lo], device_right),
               remote(buf.at[3, h, hi], buf.at[2, h, hi], device_left))
        return first, fwd

    qs = []
    for h in heads:
        mine = q_in.at[:, cols(h)]
        first, fwd = ring(mine, QB, h, z_right, z_left)
        qs.append((first, fwd, local(mine, QB.at[0, h])))
    ys = [ring(AT.at[0, h], AT, h, y_right, y_left) for h in heads]

    os = []
    for h in heads:
        first4, last4 = pl.ds(0, BLOCKS // 2), pl.ds(BLOCKS // 2, BLOCKS // 2)
        relay = (remote(OB.at[2, h, first4], RLY.at[0, h], z_right),
                 remote(LB.at[2, h, first4], LRLY.at[0, h], z_right),
                 remote(OB.at[2, h, last4], RLY.at[1, h], z_left),
                 remote(LB.at[2, h, last4], LRLY.at[1, h], z_left))
        back = (remote(OB.at[3, h], OIN.at[0, h], z_right),
                remote(LB.at[3, h], LIN.at[0, h], z_right),
                remote(OB.at[1, h], OIN.at[1, h], z_left),
                remote(LB.at[1, h], LIN.at[1, h], z_left))
        os.append((relay, back))

    rows_w = pl.ds(pl.multiple_of(c * (WIDTH // 2), WIDTH // 2), WIDTH // 2)

    def w_cols(y):
        return pl.ds(pl.multiple_of(y * FEAT, FEAT), FEAT)

    w_first = [remote(w_in.at[rows_w, w_cols(dev[1])], W.at[s, rows_w, :], dev)
               for s, dev in ((1, y_right), (3, y_left), (2, y_far))]
    w_sib = [remote(W.at[s, rows_w, :], W.at[s, rows_w, :], sibling) for s in (1, 3, 2)]
    w_own = local(w_in.at[:, w_cols(py)], W.at[0])
    cnt_copies = [remote(CB.at[0], CB.at[s], dev) for s, dev in ((1, z_right), (3, z_left), (2, z_far))]

    def flip_values(h):
        def one(j, carry):
            VB[h][j] = VIN[j, :, cols(h)].T
            return carry
        lax.fori_loop(0, BLOCKS, one, 0)

    def issue(h):
        first, _, sib_own, _, _, own = kv[h]
        go(first[0])
        go(qs[h][0])
        go([sib_own[0]])
        for copy in own + [qs[h][2]]:
            copy.start()
        flip_values(h)
        go(first[1])
        go([sib_own[1]])

    def forward(h):
        first, fwd, _, sib_near, _, _ = kv[h]
        for t in range(2):
            for side in range(2):
                first[t][side].wait_recv()
                go([fwd[t][side], sib_near[t][side]])
        for side in range(2):
            qs[h][0][side].wait_recv()
            go([qs[h][1][side]])

    def ready(h):
        _, fwd, sib_own, sib_near, sib_far, own = kv[h]
        for t in range(2):
            for side in range(2):
                fwd[t][side].wait_recv()
                go([sib_far[t][side]])
        for side in range(2):
            qs[h][1][side].wait_recv()
        for copy in own + [qs[h][2]]:
            copy.wait()
        for t in range(2):
            sib_own[t].wait_recv()
            for side in range(2):
                sib_near[t][side].wait_recv()
            for side in range(2):
                sib_far[t][side].wait_recv()

    def attend(r, h, j):
        q = QB[r, h, block_rows(j)]
        q_block = frame(px, (pz + 4 - r) % 4, c) * BLOCKS + j
        limit = CB[r, pl.ds(j, 1), :]
        scores, biases, vals = [], [], []
        for s in range(SEL):
            block = ids[s, q_block]
            xs, zs, cs = block >> 6, (block >> 4) & 3, (block >> 3) & 1
            place = ((((px + 4 - xs) & 3) * 2 + ((cs + c) & 1)) * BLOCKS) + (block & 7)
            here = jnp.where(zs == pz, 0.0, NEG)
            biases.append(jnp.where(limit > s, here, NEG))
            vals.append(VB[h][place])
            scores.append(lax.dot_general(KB[h][place], q, (((1,), (1,)), ((), ())),
                                          preferred_element_type=jnp.float32))
        if r == 0:
            biases.append(jnp.zeros((1, TILE), jnp.float32))
            vals.append(VB[h][j])
            scores.append(lax.dot_general(KB[h][j], q, (((1,), (1,)), ((), ())),
                                          preferred_element_type=jnp.float32))
        top = jnp.full((1, TILE), NEG * 0.1, jnp.float32)
        for t, b in zip(scores, biases):
            top = jnp.maximum(top, jnp.max(t, axis=0, keepdims=True) * TO_LOG2 + b)
        probs = [jnp.exp2(t * TO_LOG2 + (b - top)) for t, b in zip(scores, biases)]
        total = probs[0]
        for p in probs[1:]:
            total = total + p
        total = jnp.maximum(jnp.sum(total, axis=0, keepdims=True), 1e-30)
        o = jnp.dot(jnp.concatenate(vals, axis=1),
                    jnp.concatenate([p.astype(jnp.bfloat16) for p in probs], axis=0),
                    preferred_element_type=jnp.float32)
        return o * (1.0 / total), top + jnp.log2(total)

    def merge(parts):
        top = parts[0][1]
        for _, l in parts[1:]:
            top = jnp.maximum(top, l)
        ws = [jnp.exp2(l - top) for _, l in parts]
        mass = ws[0]
        for a in ws[1:]:
            mass = mass + a
        inv = 1.0 / mass
        o = 0.0
        for (po, _), a in zip(parts, ws):
            o = o + po.astype(jnp.float32) * (a * inv)
        return o, top + jnp.log2(mass)

    def over(first_block, n, body):
        def pair(i, carry):
            for u in range(2):
                body(first_block + i * 2 + u)
            return carry
        lax.fori_loop(0, n // 2, pair, 0)

    def block_rows(j):
        return pl.ds(pl.multiple_of(j * TILE, TILE), TILE)

    def plain(r, h):
        def body(j):
            o, l = attend(r, h, j)
            OB[r, h, j] = o.astype(jnp.bfloat16)
            LB[r, h, j] = l
        return body

    def merged(r, h, side, first_block):
        def body(j):
            o, l = merge([attend(r, h, j),
                          (RLY[side, h, j - first_block], LRLY[side, h, j - first_block])])
            OB[r, h, j] = o.astype(jnp.bfloat16)
            LB[r, h, j] = l
        return body

    def own_part(h):
        def body(j):
            o, l = attend(0, h, j)
            OWN[h, j] = o
            LB[0, h, j] = l
        return body

    def final(h):
        def body(j):
            parts = [(OWN[h, j], LB[0, h, j])]
            for side in range(2):
                parts.append((OIN[side, h, j], LIN[side, h, j]))
            o, _ = merge(parts)
            AT[0, h, block_rows(j)] = o.T.astype(jnp.bfloat16)
        return body

    def y_forward(h):
        first, fwd = ys[h]
        for side in range(2):
            first[side].wait_recv()
            go([fwd[side]])

    def project(h):
        for side in range(2):
            ys[h][1][side].wait_recv()
        last = h == HEADS_HERE - 1
        tile_n, tile_m = 256, 256

        def one(i, carry):
            cs = pl.ds(pl.multiple_of(i * tile_n, tile_n), tile_n)
            rhs = jnp.concatenate([W[r, pl.ds(h * DH, DH), cs] for r in range(RING)], axis=0)
            for m in range(TOK // tile_m):
                rs = pl.ds(m * tile_m, tile_m)
                lhs = jnp.concatenate([AT[r, h, rs] for r in range(RING)], axis=1)
                term = jnp.dot(lhs, rhs, preferred_element_type=jnp.float32)
                if h > 0:
                    term = term + ACC[rs, cs]
                if last:
                    out[rs, cs] = term.astype(jnp.bfloat16)
                else:
                    ACC[rs, cs] = term
            return carry

        lax.fori_loop(0, FEAT // tile_n, one, 0)

    values_in = local(v_in, VIN)
    values_in.start()
    for j in range(BLOCKS):
        CB[0, pl.ds(j, 1), :] = jnp.full((1, 128), cnt[j], jnp.int32)
    values_in.wait()
    issue(0)
    go(cnt_copies)
    issue(1)
    go(w_first)
    w_own.start()
    for copy in cnt_copies:
        copy.wait_recv()
    forward(0)
    issue(2)

    def finish(h):
        for copy in os[h][1]:
            copy.wait_recv()
        over(0, 8, final(h))
        go(ys[h][0])

    for h in heads:
        ready(h)
        if h + 1 < HEADS_HERE:
            forward(h + 1)
        if h + 3 < HEADS_HERE:
            issue(h + 3)
        over(0, 8, plain(2, h))
        go(os[h][0])
        if h == 1:
            for a, b in zip(w_first, w_sib):
                a.wait_recv()
                go([b])
        if h == 2:
            for copy in w_sib:
                copy.wait_recv()
            w_own.wait()
        if h > 0:
            finish(h - 1)
        if h > 1:
            project(h - 2)
        over(0, 8, own_part(h))
        over(4, 4, plain(3, h))
        over(0, 4, plain(1, h))
        for copy in os[h][0]:
            copy.wait_recv()
        over(0, 4, merged(3, h, 0, 0))
        over(4, 4, merged(1, h, 1, 4))
        go(os[h][1])
        if h > 0:
            y_forward(h - 1)
    finish(HEADS_HERE - 1)
    project(HEADS_HERE - 2)
    y_forward(HEADS_HERE - 1)
    project(HEADS_HERE - 1)
    all_waited(sent)


MESH = pl.DeviceIdType.MESH
N_REMOTE = 5 * (18 + 4 + 4 + 8) + 6 + 3
N_LOCAL = 5 * 2 + 2


def shards(queries, keys, values, block_ids, counts, w_out):
    smem = pl.BlockSpec(memory_space=pltpu.SMEM)
    vmem = pl.BlockSpec(memory_space=pltpu.VMEM)
    hbm = pl.BlockSpec(memory_space=pl.ANY)
    bf16, f32 = jnp.bfloat16, jnp.float32
    return pl.pallas_call(
        kernel,
        out_shape=jax.ShapeDtypeStruct((TOK, FEAT), bf16),
        in_specs=[smem, smem, hbm, hbm, hbm, hbm],
        out_specs=vmem,
        scratch_shapes=[
            pltpu.VMEM((4, HEADS_HERE, TOK, DH), bf16),
            pltpu.VMEM((4, BLOCKS, 128), jnp.int32),
            pltpu.VMEM((BLOCKS, TILE, WIDTH), bf16),
            pltpu.VMEM((4, HEADS_HERE, BLOCKS, DH, TILE), bf16),
            pltpu.VMEM((HEADS_HERE, BLOCKS, DH, TILE), f32),
            pltpu.VMEM((2, HEADS_HERE, BLOCKS // 2, DH, TILE), bf16),
            pltpu.VMEM((2, HEADS_HERE, BLOCKS, DH, TILE), bf16),
            pltpu.VMEM((4, HEADS_HERE, BLOCKS, 1, 128), f32),
            pltpu.VMEM((2, HEADS_HERE, BLOCKS // 2, 1, 128), f32),
            pltpu.VMEM((2, HEADS_HERE, BLOCKS, 1, 128), f32),
            pltpu.VMEM((4, HEADS_HERE, TOK, DH), bf16),
            pltpu.VMEM((4, WIDTH, FEAT), bf16),
            pltpu.VMEM((TOK, FEAT), f32),
            pltpu.SemaphoreType.DMA((N_REMOTE,)),
            pltpu.SemaphoreType.DMA((N_REMOTE,)),
            pltpu.SemaphoreType.DMA((N_LOCAL,)),
        ] + [pltpu.VMEM((8 * BLOCKS, TILE, DH), bf16)] * (2 * HEADS_HERE),
        compiler_params=pltpu.CompilerParams(
            collective_id=0, has_side_effects=True, vmem_limit_bytes=67043328),
        name="sparse_attention",
    )(block_ids.T, counts, queries, keys.reshape(BLOCKS, TILE, WIDTH), values.reshape(BLOCKS, TILE, WIDTH), w_out)


def solution(mesh):
    placed = (
        P("frames", "heads"),
        P("frames", "heads"),
        P("frames", "heads"),
        P(),
        P("frames"),
        P("heads", None),
    )
    return jax.shard_map(
        shards, mesh=mesh, in_specs=placed, out_specs=P("frames", "heads"), check_vma=False
    )
```

time: 191 us -> 169 us (0.88); the launches traced: 188 us -> 169 us
  Pallas kernels: 182 us -> 165 us
  local copies, waits for them, and re-layouts: 6.23 us -> 3.4 us
    pallas_call x1, Pallas kernels: 182 us -> 165 us  [shards(): pl.pallas_call(kernel, out_shape=jax.ShapeDtypeStruct((TOK, FEAT), bf16),...]
    unnamed x2 -> x1, local copies, waits for them, and re-layouts: 4.21 us -> 3.4 us
where the time goes in v2:
time: 169 us
  Pallas kernels  165 us (98%)
  local copies, waits for them, and re-layouts  3.4 us (2%)
    pallas_call x1, Pallas kernels, shards(): pl.pallas_call(kernel, out_shape=jax.ShapeDtypeStruct((TOK, FEAT), bf16),...  165 us
    unnamed x1, local copies, waits for them, and re-layouts  3.4 us

profile of v2, /device:TPU:0, one launch (start us, length us, event | category | flops | bytes accessed | tf_op | source)
XLA Modules:
  0.0 168.8 jit_solution(610196435780145547)
XLA Ops:
  0.0 165.4 %sparse_attention.1 = bf16[1024,1280]{1,0:T(8,128)(2,1)} custom-call(s32[4,256]{1,0:T(4,128)} %bitcast.5, s32[8]{0:T(128)} %cnt.1, bf16[1024,640]{1,0:T(8,128)(2,1)} %q_in.1, bf16[8,128,640]{2,1,0:T(8,128)(2,1)} %bitcast.3, bf16[8,128,640]{2,1,0:T(8,128)(2,1)} %bitcast.4, bf16[640,5120]{1,0:T(8,128)(2,1)} %w_in.1), custom_call_target="tpu_custom_call" | custom-call | tf_op jit(solution)/shard_map/sparse_attention/pallas_call | solution.py:377
  165.4 3.4 %copy.8 = bf16[1024,1280]{1,0:T(8,128)(2,1)} copy(bf16[1024,1280]{1,0:T(8,128)(2,1)} %sparse_attention.1) | data formatting | bytes 5242880

commit v3 on v2

--- a/solution.py
+++ b/solution.py
@@ -50,9 +50,10 @@
     x_right, x_left = (frame(up(px), pz, c), py), (frame(down(px), pz, c), py)
     z_right, z_left = (frame(px, up(pz), c), py), (frame(px, down(pz), c), py)
     z_far = (frame(px, (pz + 2) % 4, c), py)
+    x_far = (frame((px + 2) % 4, pz, c), py)
     y_right, y_left, y_far = (f, up(py)), (f, down(py)), (f, (py + 2) % 4)
     sibling = (frame(px, pz, 1 - c), py)
-    partners = [x_right, x_left, z_right, z_left, z_far, y_right, y_left, y_far, sibling]
+    partners = [x_right, x_left, z_right, z_left, x_far, z_far, y_right, y_left, y_far, sibling]
 
     barrier = pltpu.get_barrier_semaphore()
     for device in partners:
@@ -92,15 +93,20 @@
             return pl.ds(s * BLOCKS, BLOCKS)
         return pl.ds(s * BLOCKS + part * (BLOCKS // 2), BLOCKS // 2)
 
+    on_x, on_z = (x_right, x_left), (z_right, z_left)
+    kv_way = [on_x if h % 2 == 0 else on_z for h in heads]
+    q_way = [on_z if h % 2 == 0 else on_x for h in heads]
+
     kv = []
     for h in heads:
+        kv_right, kv_left = kv_way[h]
         hc = cols(h)
         first, fwd, sib_own, sib_near, sib_far, own = [], [], [], [], [], []
         for mine, buf in ((k_in.at[:, :, hc], KB[h]), (VB[h].at[slot(0)], VB[h])):
-            first.append((remote(mine, buf.at[slot(2)], x_right),
-                          remote(mine, buf.at[slot(6)], x_left)))
-            fwd.append((remote(buf.at[slot(2, 0)], buf.at[slot(4, 0)], x_right),
-                        remote(buf.at[slot(6, 1)], buf.at[slot(4, 1)], x_left)))
+            first.append((remote(mine, buf.at[slot(2)], kv_right),
+                          remote(mine, buf.at[slot(6)], kv_left)))
+            fwd.append((remote(buf.at[slot(2, 0)], buf.at[slot(4, 0)], kv_right),
+                        remote(buf.at[slot(6, 1)], buf.at[slot(4, 1)], kv_left)))
             sib_own.append(remote(mine, buf.at[slot(1)], sibling))
             sib_near.append((remote(buf.at[slot(2)], buf.at[slot(3)], sibling),
                              remote(buf.at[slot(6)], buf.at[slot(7)], sibling)))
@@ -118,22 +124,34 @@
     qs = []
     for h in heads:
         mine = q_in.at[:, cols(h)]
-        first, fwd = ring(mine, QB, h, z_right, z_left)
+        first, fwd = ring(mine, QB, h, *q_way[h])
         qs.append((first, fwd, local(mine, QB.at[0, h])))
-    ys = [ring(AT.at[0, h], AT, h, y_right, y_left) for h in heads]
+    ys = []
+    for h in heads:
+        near = [(remote(AT.at[0, h, lo], AT.at[1, h, lo], y_right),
+                 remote(AT.at[0, h, hi], AT.at[1, h, hi], y_right)),
+                (remote(AT.at[0, h, hi], AT.at[3, h, hi], y_left),
+                 remote(AT.at[0, h, lo], AT.at[3, h, lo], y_left))]
+        fwd = (remote(AT.at[1, h, lo], AT.at[2, h, lo], y_right),
+               remote(AT.at[3, h, hi], AT.at[2, h, hi], y_left))
+        ys.append((near, fwd))
 
     os = []
     for h in heads:
         first4, last4 = pl.ds(0, BLOCKS // 2), pl.ds(BLOCKS // 2, BLOCKS // 2)
-        relay = (remote(OB.at[2, h, first4], RLY.at[0, h], z_right),
-                 remote(LB.at[2, h, first4], LRLY.at[0, h], z_right),
-                 remote(OB.at[2, h, last4], RLY.at[1, h], z_left),
-                 remote(LB.at[2, h, last4], LRLY.at[1, h], z_left))
-        back = (remote(OB.at[3, h], OIN.at[0, h], z_right),
-                remote(LB.at[3, h], LIN.at[0, h], z_right),
-                remote(OB.at[1, h], OIN.at[1, h], z_left),
-                remote(LB.at[1, h], LIN.at[1, h], z_left))
-        os.append((relay, back))
+        q_right, q_left = q_way[h]
+        relay = (remote(OB.at[2, h, first4], RLY.at[0, h], q_right),
+                 remote(LB.at[2, h, first4], LRLY.at[0, h], q_right),
+                 remote(OB.at[2, h, last4], RLY.at[1, h], q_left),
+                 remote(LB.at[2, h, last4], LRLY.at[1, h], q_left))
+        back = []
+        for right_half, left_half in ((last4, first4), (first4, last4)):
+            back.append((
+                remote(OB.at[3, h, right_half], OIN.at[0, h, right_half], q_right),
+                remote(LB.at[3, h, right_half], LIN.at[0, h, right_half], q_right),
+                remote(OB.at[1, h, left_half], OIN.at[1, h, left_half], q_left),
+                remote(LB.at[1, h, left_half], LIN.at[1, h, left_half], q_left)))
+        os.append((relay, back[0], back[1]))
 
     rows_w = pl.ds(pl.multiple_of(c * (WIDTH // 2), WIDTH // 2), WIDTH // 2)
 
@@ -144,7 +162,9 @@
                for s, dev in ((1, y_right), (3, y_left), (2, y_far))]
     w_sib = [remote(W.at[s, rows_w, :], W.at[s, rows_w, :], sibling) for s in (1, 3, 2)]
     w_own = local(w_in.at[:, w_cols(py)], W.at[0])
-    cnt_copies = [remote(CB.at[0], CB.at[s], dev) for s, dev in ((1, z_right), (3, z_left), (2, z_far))]
+    cnt_copies = [remote(CB.at[0, 0], CB.at[a, s], dev)
+                  for a, devs in ((0, (z_right, z_far, z_left)), (1, (x_right, x_far, x_left)))
+                  for s, dev in zip((1, 2, 3), devs)]
 
     def flip_values(h):
         def one(j, carry):
@@ -152,33 +172,41 @@
             return carry
         lax.fori_loop(0, BLOCKS, one, 0)
 
-    def issue(h):
+    def issue_kv(h):
         first, _, sib_own, _, _, own = kv[h]
         go(first[0])
-        go(qs[h][0])
         go([sib_own[0]])
-        for copy in own + [qs[h][2]]:
+        for copy in own:
             copy.start()
         flip_values(h)
         go(first[1])
         go([sib_own[1]])
 
-    def forward(h):
+    def issue_q(h):
+        go(qs[h][0])
+        qs[h][2].start()
+
+    def forward_kv(h):
         first, fwd, _, sib_near, _, _ = kv[h]
         for t in range(2):
             for side in range(2):
                 first[t][side].wait_recv()
                 go([fwd[t][side], sib_near[t][side]])
+
+    def forward_q(h):
         for side in range(2):
             qs[h][0][side].wait_recv()
             go([qs[h][1][side]])
 
-    def ready(h):
-        _, fwd, sib_own, sib_near, sib_far, own = kv[h]
+    def share(h):
+        _, fwd, _, _, sib_far, _ = kv[h]
         for t in range(2):
             for side in range(2):
                 fwd[t][side].wait_recv()
                 go([sib_far[t][side]])
+
+    def ready(h):
+        _, _, sib_own, sib_near, sib_far, own = kv[h]
         for side in range(2):
             qs[h][1][side].wait_recv()
         for copy in own + [qs[h][2]]:
@@ -187,28 +215,31 @@
             sib_own[t].wait_recv()
             for side in range(2):
                 sib_near[t][side].wait_recv()
-            for side in range(2):
                 sib_far[t][side].wait_recv()
 
     def attend(r, h, j):
         q = QB[r, h, block_rows(j)]
-        q_block = frame(px, (pz + 4 - r) % 4, c) * BLOCKS + j
-        limit = CB[r, pl.ds(j, 1), :]
-        scores, biases, vals = [], [], []
+        if h % 2 == 0:
+            q_block = frame(px, (pz + 4 - r) % 4, c) * BLOCKS + j
+            limit = CB[0, r, pl.ds(j, 1), :]
+        else:
+            q_block = frame((px + 4 - r) % 4, pz, c) * BLOCKS + j
+            limit = CB[1 if r else 0, r, pl.ds(j, 1), :]
+        places, biases = [], []
         for s in range(SEL):
             block = ids[s, q_block]
             xs, zs, cs = block >> 6, (block >> 4) & 3, (block >> 3) & 1
-            place = ((((px + 4 - xs) & 3) * 2 + ((cs + c) & 1)) * BLOCKS) + (block & 7)
-            here = jnp.where(zs == pz, 0.0, NEG)
+            step = (px + 4 - xs) & 3 if h % 2 == 0 else (pz + 4 - zs) & 3
+            places.append((step * 2 + ((cs + c) & 1)) * BLOCKS + (block & 7))
+            here = jnp.where(zs == pz if h % 2 == 0 else xs == px, 0.0, NEG)
             biases.append(jnp.where(limit > s, here, NEG))
-            vals.append(VB[h][place])
-            scores.append(lax.dot_general(KB[h][place], q, (((1,), (1,)), ((), ())),
-                                          preferred_element_type=jnp.float32))
         if r == 0:
+            places.append(j)
             biases.append(jnp.zeros((1, TILE), jnp.float32))
-            vals.append(VB[h][j])
-            scores.append(lax.dot_general(KB[h][j], q, (((1,), (1,)), ((), ())),
-                                          preferred_element_type=jnp.float32))
+        vals = [VB[h][p] for p in places]
+        scores = lax.dot_general(jnp.concatenate([KB[h][p] for p in places], axis=0), q,
+                                 (((1,), (1,)), ((), ())), preferred_element_type=jnp.float32)
+        scores = [scores[i * TILE : (i + 1) * TILE] for i in range(len(places))]
         top = jnp.full((1, TILE), NEG * 0.1, jnp.float32)
         for t, b in zip(scores, biases):
             top = jnp.maximum(top, jnp.max(t, axis=0, keepdims=True) * TO_LOG2 + b)
@@ -236,36 +267,42 @@
             o = o + po.astype(jnp.float32) * (a * inv)
         return o, top + jnp.log2(mass)
 
-    def over(first_block, n, body):
-        def pair(i, carry):
-            for u in range(2):
-                body(first_block + i * 2 + u)
+    def over(first_block, n, body, unroll=4):
+        def some(i, carry):
+            stores = [body(first_block + i * unroll + u) for u in range(unroll)]
+            for store in stores:
+                store()
             return carry
-        lax.fori_loop(0, n // 2, pair, 0)
+        if n == unroll:
+            some(0, 0)
+        else:
+            lax.fori_loop(0, n // unroll, some, 0)
 
     def block_rows(j):
         return pl.ds(pl.multiple_of(j * TILE, TILE), TILE)
 
-    def plain(r, h):
-        def body(j):
-            o, l = attend(r, h, j)
+    def put(r, h, j, o, l):
+        def store():
             OB[r, h, j] = o.astype(jnp.bfloat16)
             LB[r, h, j] = l
-        return body
+        return store
+
+    def plain(r, h):
+        return lambda j: put(r, h, j, *attend(r, h, j))
 
     def merged(r, h, side, first_block):
-        def body(j):
-            o, l = merge([attend(r, h, j),
-                          (RLY[side, h, j - first_block], LRLY[side, h, j - first_block])])
-            OB[r, h, j] = o.astype(jnp.bfloat16)
-            LB[r, h, j] = l
-        return body
+        return lambda j: put(r, h, j, *merge([
+            attend(r, h, j),
+            (RLY[side, h, j - first_block], LRLY[side, h, j - first_block])]))
 
     def own_part(h):
         def body(j):
             o, l = attend(0, h, j)
-            OWN[h, j] = o
-            LB[0, h, j] = l
+
+            def store():
+                OWN[h, j] = o
+                LB[0, h, j] = l
+            return store
         return body
 
     def final(h):
@@ -274,18 +311,23 @@
             for side in range(2):
                 parts.append((OIN[side, h, j], LIN[side, h, j]))
             o, _ = merge(parts)
-            AT[0, h, block_rows(j)] = o.T.astype(jnp.bfloat16)
+
+            def store():
+                AT[0, h, block_rows(j)] = o.T.astype(jnp.bfloat16)
+            return store
         return body
 
     def y_forward(h):
-        first, fwd = ys[h]
+        near, fwd = ys[h]
         for side in range(2):
-            first[side].wait_recv()
+            near[side][0].wait_recv()
             go([fwd[side]])
 
     def project(h):
+        near, fwd = ys[h]
         for side in range(2):
-            ys[h][1][side].wait_recv()
+            near[side][1].wait_recv()
+            fwd[side].wait_recv()
         last = h == HEADS_HERE - 1
         tile_n, tile_m = 256, 256
 
@@ -309,63 +351,123 @@
     values_in = local(v_in, VIN)
     values_in.start()
     for j in range(BLOCKS):
-        CB[0, pl.ds(j, 1), :] = jnp.full((1, 128), cnt[j], jnp.int32)
+        CB[0, 0, pl.ds(j, 1), :] = jnp.full((1, 128), cnt[j], jnp.int32)
     values_in.wait()
-    issue(0)
-    go(cnt_copies)
-    issue(1)
-    go(w_first)
-    w_own.start()
-    for copy in cnt_copies:
-        copy.wait_recv()
-    forward(0)
-    issue(2)
-
-    def finish(h):
-        for copy in os[h][1]:
-            copy.wait_recv()
-        over(0, 8, final(h))
-        go(ys[h][0])
-
-    for h in heads:
-        ready(h)
-        if h + 1 < HEADS_HERE:
-            forward(h + 1)
-        if h + 3 < HEADS_HERE:
-            issue(h + 3)
+
+    def far_part(h):
         over(0, 8, plain(2, h))
         go(os[h][0])
-        if h == 1:
-            for a, b in zip(w_first, w_sib):
-                a.wait_recv()
-                go([b])
-        if h == 2:
-            for copy in w_sib:
-                copy.wait_recv()
-            w_own.wait()
-        if h > 0:
-            finish(h - 1)
-        if h > 1:
-            project(h - 2)
-        over(0, 8, own_part(h))
+
+    def near_part(h):
         over(4, 4, plain(3, h))
         over(0, 4, plain(1, h))
+        go(os[h][1])
+        over(0, 8, own_part(h))
+
+    def merge_part(h):
         for copy in os[h][0]:
             copy.wait_recv()
         over(0, 4, merged(3, h, 0, 0))
         over(4, 4, merged(1, h, 1, 4))
-        go(os[h][1])
-        if h > 0:
-            y_forward(h - 1)
-    finish(HEADS_HERE - 1)
-    project(HEADS_HERE - 2)
-    y_forward(HEADS_HERE - 1)
-    project(HEADS_HERE - 1)
+        go(os[h][2])
+
+    def finish(h):
+        for copy in os[h][1] + os[h][2]:
+            copy.wait_recv()
+        (right_lo, right_hi), (left_hi, left_lo) = ys[h][0]
+        over(0, 4, final(h))
+        go([right_lo])
+        over(4, 4, final(h))
+        go([left_hi, right_hi, left_lo])
+
+    def weights(step):
+        if step == 0:
+            go(cnt_copies)
+            go(w_first)
+            w_own.start()
+        elif step == 1:
+            for copy in cnt_copies:
+                copy.wait_recv()
+        elif step == 2:
+            for a, b in zip(w_first, w_sib):
+                a.wait_recv()
+                go([b])
+        else:
+            for copy in w_sib:
+                copy.wait_recv()
+            w_own.wait()
+
+    issue_q(1)
+    issue_q(2)
+    issue_q(0)
+    issue_kv(3)
+    weights(0)
+    issue_kv(0)
+    issue_kv(2)
+    forward_kv(0)
+    issue_kv(1)
+    forward_q(1)
+    forward_kv(2)
+    forward_q(0)
+    forward_kv(1)
+    issue_kv(4)
+    share(0)
+    forward_kv(3)
+    ready(0)
+    weights(1)
+    far_part(0)
+    share(1)
+    forward_q(2)
+    near_part(0)
+    ready(1)
+    share(2)
+    far_part(1)
+    near_part(1)
+    issue_q(3)
+    share(3)
+    merge_part(0)
+    ready(2)
+    near_part(2)
+    far_part(2)
+    finish(0)
+    merge_part(1)
+    issue_q(4)
+    y_forward(0)
+    forward_q(3)
+    forward_kv(4)
+    merge_part(2)
+    finish(1)
+    ready(3)
+    forward_q(4)
+    weights(2)
+    far_part(3)
+    finish(2)
+    near_part(3)
+    share(4)
+    weights(3)
+    y_forward(1)
+    merge_part(3)
+    y_forward(2)
+    ready(4)
+    far_part(4)
+    near_part(4)
+    finish(3)
+    merge_part(4)
+    project(0)
+    y_forward(3)
+    project(1)
+    finish(4)
+    project(2)
+    project(3)
+    y_forward(4)
+    project(4)
+
     all_waited(sent)
 
 
 MESH = pl.DeviceIdType.MESH
-N_REMOTE = 5 * (18 + 4 + 4 + 8) + 6 + 3
+N_REMOTE = 5 * (18 + 4 + 4 + 8) + 6 + 6
+N_REMOTE = 5 * (18 + 4 + 12 + 6) + 6 + 6
 N_LOCAL = 5 * 2 + 2
 
 
@@ -381,7 +483,7 @@
         out_specs=vmem,
         scratch_shapes=[
             pltpu.VMEM((4, HEADS_HERE, TOK, DH), bf16),
-            pltpu.VMEM((4, BLOCKS, 128), jnp.int32),
+            pltpu.VMEM((2, 4, BLOCKS, 128), jnp.int32),
             pltpu.VMEM((BLOCKS, TILE, WIDTH), bf16),
             pltpu.VMEM((4, HEADS_HERE, BLOCKS, DH, TILE), bf16),
             pltpu.VMEM((HEADS_HERE, BLOCKS, DH, TILE), f32),

time: 169 us -> 128 us (0.76)
  Pallas kernels: 165 us -> 124 us
    pallas_call x1, Pallas kernels: 165 us -> 124 us  [shards(): pl.pallas_call(kernel, out_shape=jax.ShapeDtypeStruct((TOK, FEAT), bf16),...]
where the time goes in v3:
time: 128 us; the launch traced here: 127 us
  Pallas kernels  124 us (97%)
  local copies, waits for them, and re-layouts  3.4 us (3%)
    pallas_call x1, Pallas kernels, shards(): pl.pallas_call(kernel, out_shape=jax.ShapeDtypeStruct((TOK, FEAT), bf16),...  124 us
    unnamed x1, local copies, waits for them, and re-layouts  3.4 us

profile of v3, /device:TPU:0, one launch (start us, length us, event | category | flops | bytes accessed | tf_op | source)
XLA Modules:
  0.0 127.5 jit_solution(11402252283761368215)
XLA Ops:
  0.0 124.1 %sparse_attention.1 = bf16[1024,1280]{1,0:T(8,128)(2,1)} custom-call(s32[4,256]{1,0:T(4,128)} %bitcast.5, s32[8]{0:T(128)} %cnt.1, bf16[1024,640]{1,0:T(8,128)(2,1)} %q_in.1, bf16[8,128,640]{2,1,0:T(8,128)(2,1)} %bitcast.3, bf16[8,128,640]{2,1,0:T(8,128)(2,1)} %bitcast.4, bf16[640,5120]{1,0:T(8,128)(2,1)} %w_in.1), custom_call_target="tpu_custom_call" | custom-call | tf_op jit(solution)/shard_map/sparse_attention/pallas_call | solution.py:479
  124.1 3.4 %copy.8 = bf16[1024,1280]{1,0:T(8,128)(2,1)} copy(bf16[1024,1280]{1,0:T(8,128)(2,1)} %sparse_attention.1) | data formatting | bytes 5242880

commit v4 on v3

--- a/solution.py
+++ b/solution.py
@@ -54,6 +54,11 @@
     y_right, y_left, y_far = (f, up(py)), (f, down(py)), (f, (py + 2) % 4)
     sibling = (frame(px, pz, 1 - c), py)
     partners = [x_right, x_left, z_right, z_left, x_far, z_far, y_right, y_left, y_far, sibling]
+
+    values_in = pltpu.make_async_copy(v_in, VIN, local_sem.at[N_LOCAL - 1])
+    values_in.start()
+    for j in range(BLOCKS):
+        CB[0, 0, pl.ds(j, 1), :] = jnp.full((1, 128), cnt[j], jnp.int32)
 
     barrier = pltpu.get_barrier_semaphore()
     for device in partners:
@@ -136,22 +141,38 @@
                remote(AT.at[3, h, hi], AT.at[2, h, hi], y_left))
         ys.append((near, fwd))
 
+    def pieces(h):
+        return 2 if h == HEADS_HERE - 1 else 1
+
+    def span(h):
+        return BLOCKS // 2 // pieces(h)
+
+    def piece(h, side, p):
+        return pl.ds(side * (BLOCKS // 2) + p * span(h), span(h))
+
     os = []
     for h in heads:
+        q_right, q_left = q_way[h]
+        relays, middles = [], []
+        for p in range(pieces(h)):
+            near, far = piece(h, 0, p), piece(h, 1, p)
+            place = pl.ds(p * span(h), span(h))
+            relays.append((
+                (remote(OB.at[2, h, near], RLY.at[0, h, place], q_right),
+                 remote(LB.at[2, h, near], LRLY.at[0, h, place], q_right)),
+                (remote(OB.at[2, h, far], RLY.at[1, h, place], q_left),
+                 remote(LB.at[2, h, far], LRLY.at[1, h, place], q_left))))
+            middles.append((
+                (remote(OB.at[3, h, near], OIN.at[0, h, near], q_right),
+                 remote(LB.at[3, h, near], LIN.at[0, h, near], q_right)),
+                (remote(OB.at[1, h, far], OIN.at[1, h, far], q_left),
+                 remote(LB.at[1, h, far], LIN.at[1, h, far], q_left))))
         first4, last4 = pl.ds(0, BLOCKS // 2), pl.ds(BLOCKS // 2, BLOCKS // 2)
-        q_right, q_left = q_way[h]
-        relay = (remote(OB.at[2, h, first4], RLY.at[0, h], q_right),
-                 remote(LB.at[2, h, first4], LRLY.at[0, h], q_right),
-                 remote(OB.at[2, h, last4], RLY.at[1, h], q_left),
-                 remote(LB.at[2, h, last4], LRLY.at[1, h], q_left))
-        back = []
-        for right_half, left_half in ((last4, first4), (first4, last4)):
-            back.append((
-                remote(OB.at[3, h, right_half], OIN.at[0, h, right_half], q_right),
-                remote(LB.at[3, h, right_half], LIN.at[0, h, right_half], q_right),
-                remote(OB.at[1, h, left_half], OIN.at[1, h, left_half], q_left),
-                remote(LB.at[1, h, left_half], LIN.at[1, h, left_half], q_left)))
-        os.append((relay, back[0], back[1]))
+        ends = (remote(OB.at[3, h, last4], OIN.at[0, h, last4], q_right),
+                remote(LB.at[3, h, last4], LIN.at[0, h, last4], q_right),
+                remote(OB.at[1, h, first4], OIN.at[1, h, first4], q_left),
+                remote(LB.at[1, h, first4], LIN.at[1, h, first4], q_left))
+        os.append((relays, ends, middles))
 
     rows_w = pl.ds(pl.multiple_of(c * (WIDTH // 2), WIDTH // 2), WIDTH // 2)
 
@@ -172,12 +193,17 @@
             return carry
         lax.fori_loop(0, BLOCKS, one, 0)
 
+    values_waited = []
+
     def issue_kv(h):
         first, _, sib_own, _, _, own = kv[h]
         go(first[0])
         go([sib_own[0]])
         for copy in own:
             copy.start()
+        if not values_waited:
+            values_waited.append(True)
+            values_in.wait()
         flip_values(h)
         go(first[1])
         go([sib_own[1]])
@@ -348,15 +374,14 @@
 
         lax.fori_loop(0, FEAT // tile_n, one, 0)
 
-    values_in = local(v_in, VIN)
-    values_in.start()
-    for j in range(BLOCKS):
-        CB[0, 0, pl.ds(j, 1), :] = jnp.full((1, 128), cnt[j], jnp.int32)
-    values_in.wait()
-
     def far_part(h):
-        over(0, 8, plain(2, h))
-        go(os[h][0])
+        relays = os[h][0]
+        over(0, 4, plain(2, h))
+        for relay in relays:
+            go(relay[0])
+        over(4, 4, plain(2, h))
+        for relay in relays:
+            go(relay[1])
 
     def near_part(h):
         over(4, 4, plain(3, h))
@@ -365,19 +390,28 @@
         over(0, 8, own_part(h))
 
     def merge_part(h):
-        for copy in os[h][0]:
+        relays, _, middles = os[h]
+        n = span(h)
+        for relay, middle, p in zip(relays, middles, range(pieces(h))):
+            for side, r in ((0, 3), (1, 1)):
+                for copy in relay[side]:
+                    copy.wait_recv()
+                over(side * 4 + p * n, n, merged(r, h, side, side * 4), n)
+                go(middle[side])
+
+    def finish(h):
+        _, ends, middles = os[h]
+        (right_lo, right_hi), (left_hi, left_lo) = ys[h][0]
+        n = span(h)
+        for copy in ends:
             copy.wait_recv()
-        over(0, 4, merged(3, h, 0, 0))
-        over(4, 4, merged(1, h, 1, 4))
-        go(os[h][2])
-
-    def finish(h):
-        for copy in os[h][1] + os[h][2]:
-            copy.wait_recv()
-        (right_lo, right_hi), (left_hi, left_lo) = ys[h][0]
-        over(0, 4, final(h))
-        go([right_lo])
-        over(4, 4, final(h))
+        for side in range(2):
+            for p, middle in enumerate(middles):
+                for copy in middle[side]:
+                    copy.wait_recv()
+                over(side * 4 + p * n, n, final(h), n)
+            if side == 0:
+                go([right_lo])
         go([left_hi, right_hi, left_lo])
 
     def weights(step):
@@ -397,69 +431,69 @@
                 copy.wait_recv()
             w_own.wait()
 
+    issue_q(0)
+    issue_kv(2)
+    issue_q(2)
     issue_q(1)
-    issue_q(2)
-    issue_q(0)
-    issue_kv(3)
+    issue_q(3)
+    issue_kv(1)
+    forward_kv(2)
     weights(0)
     issue_kv(0)
-    issue_kv(2)
+    forward_kv(1)
+    forward_q(2)
+    issue_kv(3)
+    weights(1)
+    forward_q(0)
+    share(1)
+    forward_q(1)
+    share(2)
+    ready(2)
+    far_part(2)
     forward_kv(0)
-    issue_kv(1)
-    forward_q(1)
-    forward_kv(2)
-    forward_q(0)
-    forward_kv(1)
+    forward_kv(3)
+    ready(1)
+    far_part(1)
     issue_kv(4)
     share(0)
-    forward_kv(3)
+    near_part(2)
+    merge_part(2)
+    share(3)
     ready(0)
-    weights(1)
     far_part(0)
-    share(1)
-    forward_q(2)
+    issue_q(4)
+    near_part(1)
+    finish(2)
+    merge_part(1)
+    forward_q(3)
+    merge_part(0)
+    weights(2)
+    forward_kv(4)
+    y_forward(2)
     near_part(0)
-    ready(1)
-    share(2)
-    far_part(1)
-    near_part(1)
-    issue_q(3)
-    share(3)
-    merge_part(0)
-    ready(2)
-    near_part(2)
-    far_part(2)
-    finish(0)
-    merge_part(1)
-    issue_q(4)
-    y_forward(0)
-    forward_q(3)
-    forward_kv(4)
-    merge_part(2)
     finish(1)
     ready(3)
+    far_part(3)
+    finish(0)
+    y_forward(1)
     forward_q(4)
-    weights(2)
-    far_part(3)
-    finish(2)
     near_part(3)
     share(4)
     weights(3)
-    y_forward(1)
     merge_part(3)
-    y_forward(2)
     ready(4)
     far_part(4)
+    y_forward(0)
     near_part(4)
     finish(3)
     merge_part(4)
+    y_forward(3)
+    finish(4)
     project(0)
-    y_forward(3)
     project(1)
-    finish(4)
     project(2)
+    y_forward(4)
     project(3)
-    y_forward(4)
     project(4)
 
     all_waited(sent)
@@ -467,7 +501,7 @@
 
 MESH = pl.DeviceIdType.MESH
 N_REMOTE = 5 * (18 + 4 + 4 + 8) + 6 + 6
-N_REMOTE = 5 * (18 + 4 + 12 + 6) + 6 + 6
+N_REMOTE = 5 * (18 + 4 + 12 + 6) + 8 + 6 + 6
 N_LOCAL = 5 * 2 + 2
 
 

time: 128 us -> 126 us (0.984)
  Pallas kernels: 124 us -> 122 us
    pallas_call x1, Pallas kernels: 124 us -> 122 us  [shards(): pl.pallas_call(kernel, out_shape=jax.ShapeDtypeStruct((TOK, FEAT), bf16),...]
where the time goes in v4:
time: 126 us
  Pallas kernels  122 us (97%)
  local copies, waits for them, and re-layouts  3.4 us (3%)
    pallas_call x1, Pallas kernels, shards(): pl.pallas_call(kernel, out_shape=jax.ShapeDtypeStruct((TOK, FEAT), bf16),...  122 us
    unnamed x1, local copies, waits for them, and re-layouts  3.4 us

profile of v4, /device:TPU:0, one launch (start us, length us, event | category | flops | bytes accessed | tf_op | source)
XLA Modules:
  0.0 125.8 jit_solution(17516969547124411719)
XLA Ops:
  0.0 122.4 %sparse_attention.1 = bf16[1024,1280]{1,0:T(8,128)(2,1)} custom-call(s32[4,256]{1,0:T(4,128)} %bitcast.5, s32[8]{0:T(128)} %cnt.1, bf16[1024,640]{1,0:T(8,128)(2,1)} %q_in.1, bf16[8,128,640]{2,1,0:T(8,128)(2,1)} %bitcast.3, bf16[8,128,640]{2,1,0:T(8,128)(2,1)} %bitcast.4, bf16[640,5120]{1,0:T(8,128)(2,1)} %w_in.1), custom_call_target="tpu_custom_call" | custom-call | tf_op jit(solution)/shard_map/sparse_attention/pallas_call | solution.py:513
  122.4 3.4 %copy.8 = bf16[1024,1280]{1,0:T(8,128)(2,1)} copy(bf16[1024,1280]{1,0:T(8,128)(2,1)} %sparse_attention.1) | data formatting | bytes 5242880
